TPU v7x, 32 devices: a whole 2x2x4 slice. The times are simulated.
32 devices in a mesh: groups: 2 (over y), tensor: 4 (over z), frames: 4 (over x, core).
Axes of the slice: x: 2, y: 2, z: 4, core: 2. Of those that a mesh axis runs over, the one named last changes fastest.
Arguments:
- patches: bfloat16 [256, 16, 3072], P('tensor', ('groups', 'frames')), parts along dimension 1, may hold values from -12 to 12
- ln_gain: float32 [3072], replicated, may hold values from 0.5 to 1.5
- in_weight: bfloat16 [3072, 4, 768], P('frames', 'tensor'), may hold values from -0.109375 to 0.109375
- q_gain: float32 [4, 128], P('tensor'), may hold values from 0.1 to 1.9
- k_gain: float32 [4, 128], P('tensor'), may hold values from 0.1 to 1.9
- out_weight: bfloat16 [4, 512, 3072], P('tensor', None, 'frames'), may hold values from -0.25 to 0.25
Outputs:
- encoded: bfloat16 [256, 16, 3072], P('tensor', ('groups', 'frames')), parts along dimension 1
There are 2 independent parts, one for each index of `groups`. A program takes and returns all parts, laid end to end along the dimension named above; an argument that names none is the same for every part. Nothing has to cross between parts.
All inputs are finite; a program needn't handle non-finite values.
Results may differ from a plain program's by a relative error of at most 0.022.
Values may be sent and summed in bfloat16 or wider, within the bound.
No kernel may reach another device: no remote copies, remote signals or barrier semaphores. Data moves between devices by JAX's collectives and lax.ppermute only.
A program may use at most 64 MiB of HBM per device.

v0:
```python
import math
import jax
import jax.numpy as jnp
from jax import lax
from jax.sharding import PartitionSpec as P


def layer_norm(values, gain_vec):
    mean_val = jnp.mean(values, axis=-1, keepdims=True)
    centered = values - mean_val
    variance = jnp.mean(centered * centered, axis=-1, keepdims=True)
    return centered * lax.rsqrt(variance + 1e-06) * gain_vec


def local(patches, ln_gain, in_weight, q_gain, k_gain, out_weight):
    head_dim = q_gain.shape[1]
    normed = layer_norm(patches.astype(jnp.float32), ln_gain).astype(jnp.bfloat16)
    in_local = in_weight[:, 0, :]
    out_local = out_weight[0]
    every_patch = lax.all_gather(normed, "tensor", axis=0, tiled=True)
    joined_cols = jnp.einsum(
        "qye,ea->qya",
        every_patch,
        lax.all_gather(in_local, "frames", axis=0, tiled=True),
        preferred_element_type=jnp.float32,
    )
    query_slice = layer_norm(joined_cols[..., :head_dim], q_gain[0])
    key_slice = layer_norm(joined_cols[..., head_dim : 2 * head_dim], k_gain[0])
    value_slice = joined_cols[..., 2 * head_dim : 3 * head_dim]
    hidden = jax.nn.gelu(joined_cols[..., 3 * head_dim :], approximate=False)
    prepared = jnp.concatenate([query_slice, key_slice, value_slice, hidden], axis=-1).astype(
        jnp.bfloat16
    )
    query_slice = prepared[..., :head_dim]
    key_slice = prepared[..., head_dim : 2 * head_dim]
    value_slice = prepared[..., 2 * head_dim : 3 * head_dim]
    attention_logits = jnp.einsum(
        "ldg,bdg->dlb", query_slice, key_slice, preferred_element_type=jnp.float32
    ) * (1.0 / math.sqrt(head_dim))
    exponent_scores = jnp.exp(attention_logits)
    softmax_total = jnp.sum(exponent_scores, axis=-1)
    attention_output = jnp.einsum(
        "jdl,ljg->djg",
        exponent_scores.astype(jnp.bfloat16),
        value_slice,
        preferred_element_type=jnp.float32,
    )
    attention_output = attention_output / jnp.transpose(softmax_total)[:, :, None]
    blended_rows = jnp.concatenate(
        [attention_output.astype(jnp.bfloat16), prepared[..., 3 * head_dim :]], axis=-1
    )
    combined_output = lax.all_gather(out_local, "frames", axis=1, tiled=True)
    summed = lax.psum_scatter(
        jnp.einsum(
            "vto,ox->vtx", blended_rows, combined_output, preferred_element_type=jnp.float32
        ).astype(jnp.bfloat16),
        "tensor",
        scatter_dimension=0,
        tiled=True,
    ).astype(jnp.float32)
    return (patches.astype(jnp.float32) + summed).astype(jnp.bfloat16)


def solution(mesh):
    return jax.shard_map(
        local,
        mesh=mesh,
        in_specs=(
            P("tensor", ("groups", "frames"), None),
            P(),
            P("frames", "tensor", None),
            P("tensor", None),
            P("tensor", None),
            P("tensor", None, "frames"),
        ),
        out_specs=P("tensor", ("groups", "frames"), None),
        check_vma=False,
    )
```

profile of v0, /device:TPU:0, one launch (start us, length us, event | category | flops | bytes accessed | tf_op | source)
XLA Modules:
  0.0 220.3 jit_solution(9089769881547310153)
XLA Ops:
  6.5 0.0 copy-start
  6.5 0.0 copy-start.1
  6.5 0.0 all-gather.6.cloned.1.call-start
  6.5 1.4 convert_reduce_fusion
  7.9 1.5 fusion.5
  9.5 0.0 copy-done
  9.5 0.0 copy-done.1
  9.5 1.2 fusion.7
  10.7 0.0 all-gather.6.cloned.1.call-update
  10.7 0.0 all-gather.8.cloned.1.call-start
  10.8 0.7 all-gather.8.cloned.1.call-update
  11.5 0.0 all-gather.10.cloned.1.call-start
  11.5 0.7 all-gather.10.cloned.1.call-update
  12.2 0.0 copy-start.2
  12.2 0.0 copy-start.3
  12.2 0.0 reduce-scatter.2.cloned.1.call-start
  12.3 64.8 %all-gather.6.cloned.1.call-done = bf16[256,2,3072]{2,0,1:T(8,128)(2,1)} async-done(((bf16[64,2,3072]{2,0,1:T(8,128)(2,1)}), bf16[256,2,3072]{2,0,1:T(8,128)(2,1)}) %all-gather.6.cloned.1.call-update) | async-done | bytes 3145744 | tf_op jit(solution)/shard_map/all_gather | solution.py:20
  77.0 37.7 %all-gather.8.cloned.1.call-done = bf16[3072,1,768]{2,0,1:T(8,128)(2,1)} async-done(((bf16[768,1,768]{2,0,1:T(8,128)(2,1)}), bf16[3072,1,768]{2,0,1:T(8,128)(2,1)}) %all-gather.8.cloned.1.call-update) | async-done | bytes 4718608 | tf_op jit(solution)/shard_map/all_gather | solution.py:24
  114.7 5.9 %fusion = f32[256,2,768]{2,0,1:T(8,128)S(1)} fusion(bf16[256,2,3072]{2,0,1:T(8,128)(2,1)} %all-gather.6.cloned.1.call-done, bf16[3072,1,768]{2,0,1:T(8,128)(2,1)} %all-gather.8.cloned.1.call-done), kind=kOutput, calls=%fused_computation | convolution fusion | flops 2415919104 | bytes 9437184 | tf_op jit(solution)/shard_map/qye,ea->qya/dot_general | solution.py:21
  120.6 0.2 slice_reduce_fusion.1
  120.8 0.4 multiply_reduce_fusion.1
  121.2 0.0 copy-done.2
  121.3 0.0 copy-done.3
  121.3 0.5 fusion.33
  121.8 0.3 fusion.11
  122.0 1.7 fusion.14
  123.8 21.1 %all-gather.10.cloned.1.call-done = bf16[1,512,3072]{2,1,0:T(8,128)(2,1)} async-done(((bf16[1,512,768]{2,1,0:T(8,128)(2,1)}), bf16[1,512,3072]{2,1,0:T(8,128)(2,1)}) %all-gather.10.cloned.1.call-update) | async-done | bytes 3145744 | tf_op jit(solution)/shard_map/all_gather | solution.py:52
  144.8 5.4 %convolution_convert_fusion = bf16[256,2,3072]{2,0,1:T(8,128)(2,1)} fusion(bf16[1,512,3072]{2,1,0:T(8,128)(2,1)} %all-gather.10.cloned.1.call-done, bf16[256,2,384]{2,0,1:T(8,128)(2,1)S(1)} %fusion.14, bf16[256,2,128]{2,0,1:T(8,128)(2,1)S(1)} %fusion.11), kind=kOutput, calls=%fused_computation.2 | convolution fusion | flops 1613234176 | bytes 6815744 | tf_op jit(solution)/shard_map/vto,ox->vtx/dot_general | solution.py:54
  150.2 0.0 reduce-scatter.2.cloned.1.call-update
  150.2 60.6 %reduce-scatter.2.cloned.1.call-done = bf16[64,2,3072]{2,0,1:T(8,128)(2,1)} async-done(((bf16[256,2,3072]{2,0,1:T(8,128)(2,1)}), bf16[64,2,3072]{2,0,1:T(8,128)(2,1)}) %reduce-scatter.2.cloned.1.call-update) | async-done | bytes 786448 | tf_op jit(solution)/shard_map/reduce_scatter | solution.py:53
  210.8 1.3 fusion.8
  212.1 1.7 copy.8
  (5 shorter events, 0.0 us)
Async XLA Ops:
  6.5 2.9 %copy-start = (bf16[64,2,3072]{2,1,0:T(2,128)(2,1)S(1)}, bf16[64,2,3072]{2,1,0:T(2,128)(2,1)}, u32[]{:S(2)}) copy-start(bf16[64,2,3072]{2,1,0:T(2,128)(2,1)} %param.6) | copy-start | bytes 2359300
  6.5 2.9 %copy-start.1 = (f32[3072]{0:T(1024)S(1)}, f32[3072]{0:T(1024)}, u32[]{:S(2)}) copy-start(f32[3072]{0:T(1024)} %param.7) | copy-start | bytes 36868
  6.5 70.5 %all-gather.6.cloned.1.call-start = ((), (), s32[]{:S(2)}) async-start(), calls=%async_computation.1 | async-start | bytes 3932160 | tf_op jit(solution)/shard_map/all_gather | solution.py:20
  10.7 104.0 %all-gather.8.cloned.1.call-start = ((), (), s32[]{:S(2)}) async-start(), calls=%async_computation.3 | async-start | bytes 5898240 | tf_op jit(solution)/shard_map/all_gather | solution.py:24
  11.5 133.3 %all-gather.10.cloned.1.call-start = ((), (), s32[]{:S(2)}) async-start(), calls=%async_computation.4 | async-start | bytes 3932160 | tf_op jit(solution)/shard_map/all_gather | solution.py:52
  12.2 109.0 %copy-start.2 = (f32[1,128]{1,0:T(1,128)S(1)}, f32[1,128]{1,0:T(1,128)}, u32[]{:S(2)}) copy-start(f32[1,128]{1,0:T(1,128)} %param.10) | copy-start | bytes 1540
  12.2 109.0 %copy-start.3 = (f32[1,128]{1,0:T(1,128)S(1)}, f32[1,128]{1,0:T(1,128)}, u32[]{:S(2)}) copy-start(f32[1,128]{1,0:T(1,128)} %param.9) | copy-start | bytes 1540
  12.2 198.5 %reduce-scatter.2.cloned.1.call-start = ((), (), s32[]{:S(2)}) async-start(), calls=%async_computation.2 | async-start | bytes 3932160 | tf_op jit(solution)/shard_map/reduce_scatter | solution.py:53
Sparse Core Ops, SparseCore 0:
  10.8 66.1 all-gather.5
  78.6 36.0 all-gather.7
  116.3 28.5 all-gather.9
  150.3 60.3 reduce-scatter.1
where the time goes:
time: 221 us; the launch traced here: 220 us
  waiting for transfers between devices  185 us (84%)
  between operations  13.2 us (6%)
  matrix products  12 us (5%)
  other arithmetic  7.81 us (4%)
    all_gather x1, waiting for transfers between devices, local(): every_patch = lax.all_gather(normed, 'tensor', axis=0, tiled=True)  64.8 us
    reduce_scatter x1, waiting for transfers between devices, local(): lax.psum_scatter(jnp.einsum('vto,ox->vtx', blended_rows, combined_output,...  60.6 us
    all_gather x1, waiting for transfers between devices, local(): lax.all_gather(in_local, 'frames', axis=0, tiled=True)  37.7 us
    all_gather x1, waiting for transfers between devices, local(): combined_output = lax.all_gather(out_local, 'frames', axis=1, tiled=True)  21.1 us
    dot_general x1, matrix products, local(): jnp.einsum('qye,ea->qya', every_patch, lax.all_gather(in_local, 'frames',...  5.89 us
    dot_general x1, matrix products, local(): jnp.einsum('vto,ox->vtx', blended_rows, combined_output, preferred_elemen...  5.36 us
  transfers between devices with their start and end apart: 4, of which 4 were waited for; matrix products, arithmetic and copies ran while one was open for 4% of the time, Pallas kernels for 0%

commit v1 on v0

--- a/solution.py
+++ b/solution.py
@@ -3,6 +3,7 @@
 import jax.numpy as jnp
 from jax import lax
 from jax.sharding import PartitionSpec as P
+from jax.lax import axis_index, axis_size, ppermute
 
 
 def layer_norm(values, gain_vec):
@@ -18,11 +19,28 @@
     in_local = in_weight[:, 0, :]
     out_local = out_weight[0]
     every_patch = lax.all_gather(normed, "tensor", axis=0, tiled=True)
-    joined_cols = jnp.einsum(
-        "qye,ea->qya",
-        every_patch,
-        lax.all_gather(in_local, "frames", axis=0, tiled=True),
-        preferred_element_type=jnp.float32,
+
+    def raise_sites(frame, net_axis, field):
+        piece_next = axis_size(net_axis)
+        r_now, shaped, field_out = (piece_next, axis_index(net_axis), frame.shape[0])
+        shelf = [(k0, (k0 + 1) % r_now) for k0 in range(r_now)]
+        s_next, raw_out = (frame, None)
+        for no in range(r_now):
+            latest = ppermute(s_next, net_axis, shelf) if no < r_now - 1 else None
+            low = field(s_next, (shaped - no) % r_now * field_out)
+            raw_out = low if raw_out is None else raw_out + low
+            s_next = latest
+        return raw_out
+
+    joined_cols = raise_sites(
+        in_local,
+        "frames",
+        lambda part, start: jnp.einsum(
+            "qye,ea->qya",
+            lax.dynamic_slice_in_dim(every_patch, start, part.shape[0], axis=2),
+            part,
+            preferred_element_type=jnp.float32,
+        ),
     )
     query_slice = layer_norm(joined_cols[..., :head_dim], q_gain[0])
     key_slice = layer_norm(joined_cols[..., head_dim : 2 * head_dim], k_gain[0])

time: 221 us -> 182 us (0.82)
  waiting for transfers between devices: 185 us -> 145 us
    all_gather x1 -> x0, waiting for transfers between devices: 37.7 us -> none  [local(): lax.all_gather(in_local, 'frames', axis=0, tiled=True)]
    all_gather x1, waiting for transfers between devices: 64.8 us -> 34.2 us  [local(): every_patch = lax.all_gather(normed, 'tensor', axis=0, tiled=True)]
    ppermute x0 -> x3, waiting for transfers between devices: none -> 30.5 us  [raise_sites(): latest = ppermute(s_next, net_axis, shelf) if no < r_now - 1 else None]
    dot_general x1 -> x4, matrix products: 5.89 us -> 6.11 us  [local(): jnp.einsum('qye,ea->qya', lax.dynamic_slice_in_dim(every_patch, start, pa...]
  transfers between devices with their start and end apart: 4 -> 6, of which waited for: 4 -> 5; matrix products, arithmetic and copies ran while one was open for 4% -> 5% of each run, Pallas kernels for 0% -> 0%
where the time goes in v1:
time: 182 us; the launch traced here: 181 us
  waiting for transfers between devices  145 us (80%)
  between operations  13.2 us (7%)
  matrix products  12.3 us (7%)
  other arithmetic  7.9 us (4%)
  local copies, waits for them, and re-layouts  2.73 us (2%)
    reduce_scatter x1, waiting for transfers between devices, local(): lax.psum_scatter(jnp.einsum('vto,ox->vtx', blended_rows, combined_output,...  60.6 us
    all_gather x1, waiting for transfers between devices, local(): every_patch = lax.all_gather(normed, 'tensor', axis=0, tiled=True)  34.2 us
    ppermute x3, waiting for transfers between devices, raise_sites(): latest = ppermute(s_next, net_axis, shelf) if no < r_now - 1 else None  30.5 us
    all_gather x1, waiting for transfers between devices, local(): combined_output = lax.all_gather(out_local, 'frames', axis=1, tiled=True)  19.4 us
    dot_general x4, matrix products, local(): jnp.einsum('qye,ea->qya', lax.dynamic_slice_in_dim(every_patch, start, pa...  6.11 us
    dot_general x1, matrix products, local(): jnp.einsum('vto,ox->vtx', blended_rows, combined_output, preferred_elemen...  5.39 us
  transfers between devices with their start and end apart: 6, of which 5 were waited for; matrix products, arithmetic and copies ran while one was open for 5% of the time, Pallas kernels for 0%

profile of v1, /device:TPU:0, one launch (start us, length us, event | category | flops | bytes accessed | tf_op | source)
XLA Modules:
  0.0 181.4 jit_solution(5927086848049520350)
XLA Ops:
  6.5 0.0 copy-start
  6.5 0.0 copy-start.2
  6.5 0.0 all-gather.4.cloned.1.call-start
  6.5 1.4 convert_reduce_fusion
  7.9 0.0 copy-start.3
  8.0 1.6 fusion.3
  9.6 0.0 copy-done
  9.6 0.0 copy-done.2
  9.6 1.2 fusion.5
  10.8 0.0 all-gather.4.cloned.1.call-update
  10.8 0.0 all-gather.6.cloned.1.call-start
  10.9 0.0 copy-done.3
  10.9 0.5 collective-permute-start
  11.4 15.8 %collective-permute-done = bf16[768,768]{1,0:T(8,128)(2,1)S(1)} collective-permute-done((bf16[768,768]{1,0:T(8,128)(2,1)S(1)}, bf16[768,768]{1,0:T(8,128)(2,1)S(1)}, u32[]{:S(2)}, u32[]{:S(2)}) %collective-permute-start) | collective-permute-done | bytes 1179680 | tf_op jit(solution)/shard_map/ppermute | solution.py:29
  27.2 0.0 copy-start.4
  27.2 0.0 collective-permute-start.1
  27.2 0.0 all-gather.6.cloned.1.call-update
  27.3 0.0 reduce-scatter.2.cloned.1.call-start
  27.3 1.0 copy-done.4
  28.3 14.7 %collective-permute-done.1 = bf16[768,768]{1,0:T(8,128)(2,1)} collective-permute-done((bf16[768,768]{1,0:T(8,128)(2,1)S(1)}, bf16[768,768]{1,0:T(8,128)(2,1)}, u32[]{:S(2)}, u32[]{:S(2)}) %collective-permute-start.1) | collective-permute-done | bytes 1179680 | tf_op jit(solution)/shard_map/ppermute | solution.py:29
  43.0 0.0 collective-permute-start.2
  43.0 34.2 %all-gather.4.cloned.1.call-done = bf16[256,2,3072]{2,0,1:T(8,128)(2,1)} async-done(((bf16[64,2,3072]{2,0,1:T(8,128)(2,1)}), bf16[256,2,3072]{2,0,1:T(8,128)(2,1)}) %all-gather.4.cloned.1.call-update) | async-done | bytes 3145744 | tf_op jit(solution)/shard_map/all_gather | solution.py:21
  77.1 0.0 copy-start.1
  77.1 2.4 %fusion.9 = f32[256,2,768]{2,0,1:T(8,128)S(1)} fusion(bf16[768,768]{1,0:T(8,128)(2,1)} %collective-permute-done.1, bf16[256,2,3072]{2,0,1:T(8,128)(2,1)} %all-gather.4.cloned.1.call-done, s32[]{:T(128)S(6)} %select_n.36), kind=kOutput, calls=%fused_computation.16 | convolution fusion | flops 603979776 | bytes 3538948 | tf_op jit(solution)/shard_map/qye,ea->qya/dot_general | solution.py:38
  79.6 0.0 copy-done.1
  79.6 2.1 %fusion.11 = f32[256,2,768]{2,0,1:T(8,128)S(1)} fusion(bf16[768,768]{1,0:T(8,128)(2,1)} %copy-done.4, bf16[256,2,3072]{2,0,1:T(8,128)(2,1)S(1)} %copy-done.1, s32[]{:T(128)S(6)} %select_n.34), kind=kOutput, calls=%fused_computation.18 | convolution fusion | flops 603979776 | bytes 3538948 | tf_op jit(solution)/shard_map/qye,ea->qya/dot_general | solution.py:38
  81.7 0.8 fusion.13
  82.5 0.0 copy-start.5
  82.5 0.0 copy-start.6
  82.5 0.0 collective-permute-done.2
  82.5 0.8 add_add_fusion
  83.3 0.2 slice_reduce_fusion.1
  83.6 0.4 multiply_reduce_fusion.1
  84.0 0.0 copy-done.5
  84.0 0.0 copy-done.6
  84.0 0.5 fusion.46
  84.5 0.3 fusion.16
  84.8 1.7 fusion.19
  86.5 19.4 %all-gather.6.cloned.1.call-done = bf16[1,512,3072]{2,1,0:T(8,128)(2,1)} async-done(((bf16[1,512,768]{2,1,0:T(8,128)(2,1)}), bf16[1,512,3072]{2,1,0:T(8,128)(2,1)}) %all-gather.6.cloned.1.call-update) | async-done | bytes 3145744 | tf_op jit(solution)/shard_map/all_gather | solution.py:70
  105.9 5.4 %convolution_convert_fusion = bf16[256,2,3072]{2,0,1:T(8,128)(2,1)} fusion(bf16[1,512,3072]{2,1,0:T(8,128)(2,1)} %all-gather.6.cloned.1.call-done, bf16[256,2,384]{2,0,1:T(8,128)(2,1)S(1)} %fusion.19, bf16[256,2,128]{2,0,1:T(8,128)(2,1)S(1)} %fusion.16), kind=kOutput, calls=%fused_computation | convolution fusion | flops 1613234176 | bytes 6815744 | tf_op jit(solution)/shard_map/vto,ox->vtx/dot_general | solution.py:72
  111.3 0.0 reduce-scatter.2.cloned.1.call-update
  111.3 60.6 %reduce-scatter.2.cloned.1.call-done = bf16[64,2,3072]{2,0,1:T(8,128)(2,1)} async-done(((bf16[256,2,3072]{2,0,1:T(8,128)(2,1)}), bf16[64,2,3072]{2,0,1:T(8,128)(2,1)}) %reduce-scatter.2.cloned.1.call-update) | async-done | bytes 786448 | tf_op jit(solution)/shard_map/reduce_scatter | solution.py:71
  171.9 1.3 fusion.6
  173.2 1.7 copy.8
  (5 shorter events, 0.0 us)
Async XLA Ops:
  6.5 3.0 %copy-start = (bf16[64,2,3072]{2,1,0:T(2,128)(2,1)S(1)}, bf16[64,2,3072]{2,1,0:T(2,128)(2,1)}, u32[]{:S(2)}) copy-start(bf16[64,2,3072]{2,1,0:T(2,128)(2,1)} %param.6) | copy-start | bytes 2359300
  6.5 3.0 %copy-start.2 = (f32[3072]{0:T(1024)S(1)}, f32[3072]{0:T(1024)}, u32[]{:S(2)}) copy-start(f32[3072]{0:T(1024)} %param.7) | copy-start | bytes 36868
  6.5 70.6 %all-gather.4.cloned.1.call-start = ((), (), s32[]{:S(2)}) async-start(), calls=%async_computation.1 | async-start | bytes 3932160 | tf_op jit(solution)/shard_map/all_gather | solution.py:21
  7.9 2.9 %copy-start.3 = (bf16[768,1,768]{2,0,1:T(8,128)(2,1)S(1)}, bf16[768,1,768]{2,0,1:T(8,128)(2,1)}, u32[]{:S(2)}) copy-start(bf16[768,1,768]{2,0,1:T(8,128)(2,1)} %param.8) | copy-start | bytes 3538948
  10.8 95.1 %all-gather.6.cloned.1.call-start = ((), (), s32[]{:S(2)}) async-start(), calls=%async_computation.3 | async-start | bytes 3932160 | tf_op jit(solution)/shard_map/all_gather | solution.py:70
  10.9 16.3 %collective-permute-start = (bf16[768,768]{1,0:T(8,128)(2,1)S(1)}, bf16[768,768]{1,0:T(8,128)(2,1)S(1)}, u32[]{:S(2)}, u32[]{:S(2)}) collective-permute-start(bf16[768,768]{1,0:T(8,128)(2,1)S(1)} %bitcast.27), channel_id=1, source_target_pairs={{0,1},{1,2},{2,3},{3,0},{4,5},{5,6},{6,7},{7,4},{8,9},{9,10},{10,1... | collective-permute-start | bytes 3538952 | tf_op jit(solution)/shard_map/ppermute | solution.py:29
  27.2 1.1 copy-start.4
  27.2 15.7 %collective-permute-start.1 = (bf16[768,768]{1,0:T(8,128)(2,1)S(1)}, bf16[768,768]{1,0:T(8,128)(2,1)}, u32[]{:S(2)}, u32[]{:S(2)}) collective-permute-start(bf16[768,768]{1,0:T(8,128)(2,1)S(1)} %collective-permute-done), channel_id=1, source_target_pairs={{0,1},{1,2},{2,3},{3,0},{4,5},{5,6},{6,7},{7,4},{8,9},{9,10},{10,1... | collective-permute-start | bytes 3538952 | tf_op jit(solution)/shard_map/ppermute | solution.py:29
  27.3 144.6 %reduce-scatter.2.cloned.1.call-start = ((), (), s32[]{:S(2)}) async-start(), calls=%async_computation.2 | async-start | bytes 3932160 | tf_op jit(solution)/shard_map/reduce_scatter | solution.py:71
  43.0 39.5 %collective-permute-start.2 = (bf16[768,768]{1,0:T(8,128)(2,1)}, bf16[768,768]{1,0:T(8,128)(2,1)S(1)}, u32[]{:S(2)}, u32[]{:S(2)}) collective-permute-start(bf16[768,768]{1,0:T(8,128)(2,1)} %collective-permute-done.1), channel_id=1, source_target_pairs={{0,1},{1,2},{2,3},{3,0},{4,5},{5,6},{6,7},{7,4},{8,9},{9,10},{10,1... | collective-permute-start | bytes 3538952 | tf_op jit(solution)/shard_map/ppermute | solution.py:29
  77.1 2.5 %copy-start.1 = (bf16[256,2,3072]{2,0,1:T(8,128)(2,1)S(1)}, bf16[256,2,3072]{2,0,1:T(8,128)(2,1)}, u32[]{:S(2)}) copy-start(bf16[256,2,3072]{2,0,1:T(8,128)(2,1)} %all-gather.4.cloned.1.call-done) | copy-start | bytes 9437188
  82.5 1.5 copy-start.5
  82.5 1.5 copy-start.6
Sparse Core Ops, SparseCore 0:
  10.9 66.1 all-gather.3
  78.7 27.1 all-gather.5
  111.4 60.3 reduce-scatter.1
